TPU v7x, 128 devices: a whole 4x4x4 slice. The times are simulated.
128 devices in a mesh: rep: 16 (over y, x_hi, core), fsdp: 8 (over x_lo, z).
Axes of the slice: x: 4 (x_hi: 2, x_lo: 2; x = x_hi * 2 + x_lo), y: 4, z: 4, core: 2. Of those that a mesh axis runs over, the one named last changes fastest.
Arguments:
- replica_inner_weight: bfloat16 [16, 1024, 16384], P('rep', 'fsdp'), may hold values from -30 to 30
- outer_weights: float32 [1024, 16384], P('fsdp'), may hold values from -6 to 6
- momentum: float32 [1024, 16384], P('fsdp', 'rep'), may hold values from -4 to 4
- exponents: int32 [16, 1024, 128], P('rep', 'fsdp'), may hold values from 0 to 2
- levels: int32 [16], replicated, may hold values from -60 to 60, as said below
Outputs:
- inner_next: bfloat16 [16, 1024, 16384], P('rep', 'fsdp')
- momentum_next: float32 [1024, 16384], P('fsdp', 'rep')
- outer_next: float32 [1024, 16384], P('fsdp', 'rep')
Inputs may be any that keep to these rules, and one draw needn't show every extreme that they name: `levels`: 16 distinct values, half of them negative and half positive, ascending.
All inputs are finite; a program needn't handle non-finite values. Where the computation divides by a largest or mean magnitude, that divisor is 1e-20 or more.
Results may differ from a plain program's by a relative error of at most 0.0085.
Values may be sent and summed in bfloat16 or wider, within the bound.
No kernel may reach another device: no remote copies, remote signals or barrier semaphores. Data moves between devices by JAX's collectives and lax.ppermute only.
A program may use at most 128 MiB of HBM per device.

v0:
```python
import jax
import jax.numpy as jnp
from jax import lax
from jax.sharding import Mesh
from jax.sharding import PartitionSpec as P

NLEV = 16
REP = ("rep_0", "rep_1", "rep_2")
FSDP = ("fsdp_0", "fsdp_1")
REP_FSDP = ("rep_0", "rep_1", "rep_2", "fsdp_0", "fsdp_1")
softness_factor = 0.02
clip_rms = 0.1
outer_rate = 0.7
outer_mu = 0.9
mix_rate = 0.5


def by_axis(array, axes):
    for axis in axes:
        array = lax.psum(array, axis)
    return array


def encode_grad(pseudo_grad, exponents, levels):
    quantize_grid_points = levels.astype(jnp.float32) / jnp.max(jnp.abs(levels)).astype(jnp.float32)
    block_scale = jnp.exp2(exponents.astype(jnp.float32))[..., None]
    row_count = pseudo_grad.shape[0]
    rescaled_gradient = pseudo_grad.reshape(row_count, exponents.shape[-1], -1) / block_scale
    closest_grid_level = (rescaled_gradient - quantize_grid_points[0]) ** 2
    for grid_level_index in range(1, NLEV):
        closest_grid_level = jnp.minimum(
            closest_grid_level, (rescaled_gradient - quantize_grid_points[grid_level_index]) ** 2
        )
    weighted = jnp.zeros_like(rescaled_gradient)
    weights_sum = jnp.zeros_like(rescaled_gradient)
    for grid_level_index in range(NLEV):
        current_weight = jnp.exp(
            -(
                (rescaled_gradient - quantize_grid_points[grid_level_index]) ** 2
                - closest_grid_level
            )
            / softness_factor
        )
        weighted = weighted + current_weight * quantize_grid_points[grid_level_index]
        weights_sum = weights_sum + current_weight
    coded = block_scale * weighted / weights_sum
    return coded.reshape(row_count, -1).astype(jnp.bfloat16)


def clip_factor(squares, entries):
    return jnp.minimum(
        jnp.float32(1.0), clip_rms / jnp.sqrt(squares / jnp.float32(entries) + 1e-06)
    )


def per_device(replica_inner_weight, outer_weights, momentum, exponents, levels):
    replicas = lax.axis_size(REP)
    row_count, columns = outer_weights.shape
    entries = row_count * lax.axis_size(FSDP) * columns
    width = momentum.shape[1]
    start = lax.axis_index(REP) * width
    coded = encode_grad(
        outer_weights - replica_inner_weight[0].astype(jnp.float32), exponents[0], levels
    )
    share = lax.psum_scatter(coded, REP, scatter_dimension=1, tiled=True).astype(jnp.float32)
    mean_grad = share / jnp.float32(replicas)
    squares = by_axis(jnp.sum(mean_grad * mean_grad), REP_FSDP)
    grad = clip_factor(squares, entries) * mean_grad
    momentum_next = outer_mu * momentum + grad
    outer_piece = lax.dynamic_slice_in_dim(outer_weights, start, width, 1)
    outer_next = outer_piece - outer_rate * (grad + outer_mu * momentum_next)
    outer_half = lax.all_gather(outer_next.astype(jnp.bfloat16), REP, axis=1, tiled=True)
    mixed = mix_rate * outer_half.astype(jnp.float32) + (1.0 - mix_rate) * replica_inner_weight[
        0
    ].astype(jnp.float32)
    inner_next = mixed.astype(jnp.bfloat16)[None]
    return (inner_next, momentum_next, outer_next)


def solution(mesh):
    torus = Mesh(
        mesh.devices.reshape(4, 2, 2, 2, 4), ("rep_0", "rep_1", "rep_2", "fsdp_0", "fsdp_1")
    )
    placed = (P(REP, FSDP, None), P(FSDP, None), P(FSDP, REP), P(REP, FSDP, None), P())
    return jax.shard_map(
        per_device,
        mesh=torus,
        in_specs=placed,
        out_specs=(P(REP, FSDP, None), P(FSDP, REP), P(FSDP, REP)),
        check_vma=False,
    )
```

profile of v0, /device:TPU:1, one launch (start us, length us, event | category | flops | bytes accessed | tf_op | source)
XLA Modules:
  0.0 264.6 jit_solution(7247658938995126674)
XLA Ops:
  7.2 0.0 reduce-scatter.2.cloned.1.call-start
  7.2 1.3 abs_reduce_fusion
  9.2 0.0 copy-start
  9.2 0.8 convert_divide_fusion
  10.0 0.7 fusion.15
  10.7 0.9 exponential_bitcast_fusion
  11.6 2.3 mul.130
  13.9 0.0 copy-done
  13.9 0.0 copy-start.1
  13.9 60.4 %fusion.4 = bf16[128,16384]{1,0:T(8,128)(2,1)} fusion(f32[128,16384]{1,0:T(8,128)} %param.6, f32[16,8,128,128]{3,2,1,0:T(8,128)S(1)} %bitcast.34, bf16[1,128,16384]{2,1,0:T(8,128)(2,1)S(1)} %copy-done, f32[]{:T(128)} %bitcast.17, f32[]{:T(128)} %bitcast.16, f32[]{:T(128)} %bitcast.15, f32[]{:T(128)} %bitcast.14, f32[]{:T(128)} %bitcast.13, f32[]{:T(128)} %bitcast.12, ...), kind=kLoop, calls=%fused_computation.7 | loop fusion | flops 308281344 | bytes 25165888 | tf_op jit(solution)/shard_map/convert_element_type | solution.py:47
  74.3 0.0 reduce-scatter.2.cloned.1.call-update
  74.3 0.0 all-gather.2.cloned.1.call-start
  74.4 82.5 %reduce-scatter.2.cloned.1.call-done = bf16[128,1024]{1,0:T(8,128)(2,1)} async-done(((bf16[128,16384]{1,0:T(8,128)(2,1)}), bf16[128,1024]{1,0:T(8,128)(2,1)}) %reduce-scatter.2.cloned.1.call-update) | async-done | bytes 262160 | tf_op jit(solution)/shard_map/reduce_scatter | solution.py:65
  156.9 1.7 fusion.11
  158.5 8.7 %psum.35 = f32[]{:T(128)} all-reduce(f32[]{:T(128)} %fusion.11), channel_id=1, replica_groups=mesh['rep_0'=4,'rep_1'=2,'rep_2'=2,'fsdp_0'=2,'fsdp_1'=4] {'rep_0'}, use_global_device_ids=true, to_apply=%region_3.0 | all-reduce | flops 1 | bytes 8 | tf_op jit(solution)/shard_map/psum | solution.py:20
  167.3 5.9 %psum.36 = f32[]{:T(128)} all-reduce(f32[]{:T(128)} %psum.35), channel_id=1, replica_groups=mesh['rep_0'=4,'rep_1'=2,'rep_2'=2,'fsdp_0'=2,'fsdp_1'=4] {'rep_1'}, use_global_device_ids=true, to_apply=%region_4.0 | all-reduce | flops 1 | bytes 8 | tf_op jit(solution)/shard_map/psum | solution.py:20
  173.2 7.9 %psum.37 = f32[]{:T(128)} all-reduce(f32[]{:T(128)} %psum.36), channel_id=1, replica_groups=mesh['rep_0'=4,'rep_1'=2,'rep_2'=2,'fsdp_0'=2,'fsdp_1'=4] {'rep_2'}, use_global_device_ids=true, to_apply=%region_5.0 | all-reduce | flops 1 | bytes 8 | tf_op jit(solution)/shard_map/psum | solution.py:20
  181.1 4.4 %psum.38 = f32[]{:T(128)} all-reduce(f32[]{:T(128)} %psum.37), channel_id=1, replica_groups=mesh['rep_0'=4,'rep_1'=2,'rep_2'=2,'fsdp_0'=2,'fsdp_1'=4] {'fsdp_0'}, use_global_device_ids=true, to_apply=%region_6.0 | all-reduce | flops 1 | bytes 8 | tf_op jit(solution)/shard_map/psum | solution.py:20
  185.5 9.3 %psum.39 = f32[]{:T(128)} all-reduce(f32[]{:T(128)} %psum.38), channel_id=1, replica_groups=mesh['rep_0'=4,'rep_1'=2,'rep_2'=2,'fsdp_0'=2,'fsdp_1'=4] {'fsdp_1'}, use_global_device_ids=true, to_apply=%region_7.0 | all-reduce | flops 1 | bytes 8 | tf_op jit(solution)/shard_map/psum | solution.py:20
  195.4 0.0 copy-done.1
  195.4 2.3 fusion.12
  197.8 0.0 all-gather.2.cloned.1.call-update
  197.8 53.3 %all-gather.2.cloned.1.call-done = bf16[128,16384]{1,0:T(8,128)(2,1)} async-done(((bf16[128,1024]{1,0:T(8,128)(2,1)}), bf16[128,16384]{1,0:T(8,128)(2,1)}) %all-gather.2.cloned.1.call-update) | async-done | bytes 4194320 | tf_op jit(solution)/shard_map/all_gather | solution.py:72
  251.1 6.7 %fusion.5 = bf16[1,128,16384]{2,1,0:T(8,128)(2,1)} fusion(bf16[128,16384]{1,0:T(8,128)(2,1)} %all-gather.2.cloned.1.call-done, bf16[1,128,16384]{2,1,0:T(8,128)(2,1)} %param.5), kind=kLoop, calls=%fused_computation.8 | loop fusion | flops 10485760 | bytes 12582912 | tf_op jit(solution)/shard_map/broadcast_in_dim | solution.py:76
Async XLA Ops:
  7.2 149.7 %reduce-scatter.2.cloned.1.call-start = ((), (), s32[]{:S(2)}) async-start(), calls=%async_computation.1 | async-start | bytes 4456448 | tf_op jit(solution)/shard_map/reduce_scatter | solution.py:65
  9.2 4.7 %copy-start = (bf16[1,128,16384]{2,1,0:T(8,128)(2,1)S(1)}, bf16[1,128,16384]{2,1,0:T(8,128)(2,1)}, u32[]{:S(2)}) copy-start(bf16[1,128,16384]{2,1,0:T(8,128)(2,1)} %param.5) | copy-start | bytes 12582916
  13.9 181.5 %copy-start.1 = (f32[128,1024]{1,0:T(8,128)S(1)}, f32[128,1024]{1,0:T(8,128)}, u32[]{:S(2)}) copy-start(f32[128,1024]{1,0:T(8,128)} %param.7) | copy-start | bytes 1572868
  74.3 176.8 %all-gather.2.cloned.1.call-start = ((), (), s32[]{:S(2)}) async-start(), calls=%async_computation.2 | async-start | bytes 4456448 | tf_op jit(solution)/shard_map/all_gather | solution.py:72
Sparse Core Ops, SparseCore 0:
  74.4 82.3 reduce-scatter.1
  197.9 53.0 all-gather.1
where the time goes:
time: 265 us
  waiting for transfers between devices  136 us (51%)
  other arithmetic  74.1 us (28%)
  blocking collectives  36.2 us (14%)
  between operations  15.4 us (6%)
  local copies, waits for them, and re-layouts  3.03 us (1%)
    reduce_scatter x1, waiting for transfers between devices, per_device(): lax.psum_scatter(coded, REP, scatter_dimension=1, tiled=True)  82.5 us
    convert_element_type x1, other arithmetic, encode_grad(): return coded.reshape(row_count, -1).astype(jnp.bfloat16)  60.4 us
    all_gather x1, waiting for transfers between devices, per_device(): lax.all_gather(outer_next.astype(jnp.bfloat16), REP, axis=1, tiled=True)  53.3 us
    psum x5, blocking collectives, by_axis(): array = lax.psum(array, axis)  36.2 us
    broadcast_in_dim x1, other arithmetic, per_device(): inner_next = mixed.astype(jnp.bfloat16)[None]  6.7 us
  transfers between devices with their start and end apart: 2, of which 2 were waited for; matrix products, arithmetic and copies ran while one was open for 0% of the time, Pallas kernels for 0%

commit v1 on v0

--- a/solution.py
+++ b/solution.py
@@ -69,7 +69,11 @@
     momentum_next = outer_mu * momentum + grad
     outer_piece = lax.dynamic_slice_in_dim(outer_weights, start, width, 1)
     outer_next = outer_piece - outer_rate * (grad + outer_mu * momentum_next)
-    outer_half = lax.all_gather(outer_next.astype(jnp.bfloat16), REP, axis=1, tiled=True)
+    block = outer_next.astype(jnp.bfloat16)
+    devices = lax.axis_size(REP)
+    tiles = jnp.stack([block for _ in range(devices)])
+    tiles = lax.all_to_all(tiles, REP, split_axis=0, concat_axis=0)
+    outer_half = jnp.concatenate(tiles, axis=1)
     mixed = mix_rate * outer_half.astype(jnp.float32) + (1.0 - mix_rate) * replica_inner_weight[
         0
     ].astype(jnp.float32)

time: 265 us -> 295 us (1.11)
  local copies, waits for them, and re-layouts: 3.03 us -> 34 us
  starting transfers between devices: 0.08 us -> 7.81 us
  other arithmetic: 74.1 us -> 69.1 us
  waiting for transfers between devices: 136 us -> 132 us
    all_gather x1 -> x0, waiting for transfers between devices: 53.3 us -> none  [per_device(): lax.all_gather(outer_next.astype(jnp.bfloat16), REP, axis=1, tiled=True)]
    all_to_all x0 -> x1, waiting for transfers between devices: none -> 49 us  [per_device(): tiles = lax.all_to_all(tiles, REP, split_axis=0, concat_axis=0)]
    unnamed x4 -> x10, local copies, waits for them, and re-layouts: 0.01 us -> 24.2 us
    all_to_all x0 -> x1, starting transfers between devices: none -> 7.78 us  [per_device(): tiles = lax.all_to_all(tiles, REP, split_axis=0, concat_axis=0)]
    broadcast_in_dim x1 -> x0, other arithmetic: 6.7 us -> none  [per_device(): inner_next = mixed.astype(jnp.bfloat16)[None]]
    all_to_all x0 -> x1, local copies, waits for them, and re-layouts: none -> 6.4 us  [per_device(): tiles = lax.all_to_all(tiles, REP, split_axis=0, concat_axis=0)]
    convert_element_type x1 -> x3, other arithmetic: 2.35 us -> 6.93 us  [the longest x1 3.18 us: per_device(): outer_half.astype(jnp.float32)]
  transfers between devices with their start and end apart: 2 -> 2, of which waited for: 2 -> 2; matrix products, arithmetic and copies ran while one was open for 0% -> 1% of each run, Pallas kernels for 0% -> 0%
where the time goes in v1:
time: 295 us; the launch traced here: 294 us
  waiting for transfers between devices  132 us (45%)
  other arithmetic  69.1 us (23%)
  blocking collectives  36.2 us (12%)
  local copies, waits for them, and re-layouts  34 us (12%)
  between operations  15.4 us (5%)
  starting transfers between devices  7.81 us (3%)
    reduce_scatter x1, waiting for transfers between devices, per_device(): lax.psum_scatter(coded, REP, scatter_dimension=1, tiled=True)  82.6 us
    convert_element_type x1, other arithmetic, encode_grad(): return coded.reshape(row_count, -1).astype(jnp.bfloat16)  57.6 us
    all_to_all x1, waiting for transfers between devices, per_device(): tiles = lax.all_to_all(tiles, REP, split_axis=0, concat_axis=0)  49 us
    psum x5, blocking collectives, by_axis(): array = lax.psum(array, axis)  36.2 us
    unnamed x10, local copies, waits for them, and re-layouts  24.2 us
    all_to_all x1, starting transfers between devices, per_device(): tiles = lax.all_to_all(tiles, REP, split_axis=0, concat_axis=0)  7.78 us
    all_to_all x1, local copies, waits for them, and re-layouts, per_device(): tiles = lax.all_to_all(tiles, REP, split_axis=0, concat_axis=0)  6.4 us
  transfers between devices with their start and end apart: 2, of which 2 were waited for; matrix products, arithmetic and copies ran while one was open for 1% of the time, Pallas kernels for 0%

profile of v1, /device:TPU:1, one launch (start us, length us, event | category | flops | bytes accessed | tf_op | source)
XLA Modules:
  0.0 294.1 jit_solution(3181373066065009256)
XLA Ops:
  7.2 0.0 reduce-scatter.2.cloned.1.call-start
  7.2 1.3 abs_reduce_fusion
  9.2 0.7 convert_divide_fusion
  9.8 0.7 fusion.13
  10.5 0.9 exponential_bitcast_fusion
  11.4 0.1 copy.9
  11.5 6.4 %copy.10 = bf16[1,128,16384]{1,2,0:T(8,128)(2,1)} copy(bf16[1,128,16384]{2,1,0:T(8,128)(2,1)} %param.5) | data formatting | bytes 8388608 | tf_op args[0]
  17.8 9.0 %copy.8 = f32[128,16384]{0,1:T(8,128)} copy(f32[128,16384]{1,0:T(8,128)} %param.6) | data formatting | bytes 16777216 | tf_op args[1]
  26.8 0.0 copy-start.1
  26.8 57.6 %fusion.4 = bf16[128,16384]{0,1:T(8,128)(2,1)} fusion(f32[128,16384]{0,1:T(8,128)} %copy.8, bf16[1,128,16384]{1,2,0:T(8,128)(2,1)} %copy.10, f32[]{:T(128)} %bitcast.18, f32[]{:T(128)} %bitcast.17, f32[]{:T(128)} %bitcast.16, f32[]{:T(128)} %bitcast.15, f32[]{:T(128)} %bitcast.14, f32[]{:T(128)} %bitcast.13, f32[]{:T(128)} %bitcast.12, f32[]{:T(128)} %bitcast.11, ...), kind=kLoop, calls=%fused_computation.8 | loop fusion | flops 308281344 | bytes 16842816 | tf_op jit(solution)/shard_map/convert_element_type | solution.py:47
  84.5 0.0 reduce-scatter.2.cloned.1.call-update
  84.5 82.6 %reduce-scatter.2.cloned.1.call-done = bf16[128,1024]{0,1:T(8,128)(2,1)} async-done(((bf16[128,16384]{0,1:T(8,128)(2,1)}), bf16[128,1024]{0,1:T(8,128)(2,1)}) %reduce-scatter.2.cloned.1.call-update) | async-done | bytes 262160 | tf_op jit(solution)/shard_map/reduce_scatter | solution.py:65
  167.1 1.7 fusion.10
  168.8 8.7 %psum.35 = f32[]{:T(128)} all-reduce(f32[]{:T(128)} %fusion.10), channel_id=1, replica_groups=mesh['rep_0'=4,'rep_1'=2,'rep_2'=2,'fsdp_0'=2,'fsdp_1'=4] {'rep_0'}, use_global_device_ids=true, to_apply=%region_3.0 | all-reduce | flops 1 | bytes 8 | tf_op jit(solution)/shard_map/psum | solution.py:20
  177.5 5.9 %psum.36 = f32[]{:T(128)} all-reduce(f32[]{:T(128)} %psum.35), channel_id=1, replica_groups=mesh['rep_0'=4,'rep_1'=2,'rep_2'=2,'fsdp_0'=2,'fsdp_1'=4] {'rep_1'}, use_global_device_ids=true, to_apply=%region_4.0 | all-reduce | flops 1 | bytes 8 | tf_op jit(solution)/shard_map/psum | solution.py:20
  183.4 7.9 %psum.37 = f32[]{:T(128)} all-reduce(f32[]{:T(128)} %psum.36), channel_id=1, replica_groups=mesh['rep_0'=4,'rep_1'=2,'rep_2'=2,'fsdp_0'=2,'fsdp_1'=4] {'rep_2'}, use_global_device_ids=true, to_apply=%region_5.0 | all-reduce | flops 1 | bytes 8 | tf_op jit(solution)/shard_map/psum | solution.py:20
  191.3 0.0 copy-done.1
  191.3 0.2 copy.12
  191.5 4.4 %psum.38 = f32[]{:T(128)} all-reduce(f32[]{:T(128)} %psum.37), channel_id=1, replica_groups=mesh['rep_0'=4,'rep_1'=2,'rep_2'=2,'fsdp_0'=2,'fsdp_1'=4] {'fsdp_0'}, use_global_device_ids=true, to_apply=%region_6.0 | all-reduce | flops 1 | bytes 8 | tf_op jit(solution)/shard_map/psum | solution.py:20
  195.9 9.3 %psum.39 = f32[]{:T(128)} all-reduce(f32[]{:T(128)} %psum.38), channel_id=1, replica_groups=mesh['rep_0'=4,'rep_1'=2,'rep_2'=2,'fsdp_0'=2,'fsdp_1'=4] {'fsdp_1'}, use_global_device_ids=true, to_apply=%region_7.0 | all-reduce | flops 1 | bytes 8 | tf_op jit(solution)/shard_map/psum | solution.py:20
  205.9 1.3 fusion.11
  207.2 0.1 copy.13
  207.3 2.5 stack.2
  209.8 7.8 %all-to-all-start = ((bf16[16,128,1024]{2,1,0:T(8,128)(2,1)}), bf16[16,128,1024]{2,1,0:T(8,128)(2,1)}, u32[]{:S(2)}, u32[]{:S(2)}) async-start(bf16[16,128,1024]{2,1,0:T(8,128)(2,1)} %stack.2), calls=%async_computation.1 | async-start | bytes 8388608 | tf_op jit(solution)/shard_map/all_to_all | solution.py:75
  217.6 1.0 copy.17
  218.6 1.0 copy.16
  219.6 49.0 %all-to-all-done = bf16[16,128,1024]{2,1,0:T(8,128)(2,1)} async-done(((bf16[16,128,1024]{2,1,0:T(8,128)(2,1)}), bf16[16,128,1024]{2,1,0:T(8,128)(2,1)}, u32[]{:S(2)}, u32[]{:S(2)}) %all-to-all-start) | async-done | bytes 4194336 | tf_op jit(solution)/shard_map/all_to_all | solution.py:75
  268.6 6.4 %copy.14 = bf16[16,128,1024]{1,2,0:T(8,128)(2,1)} copy(bf16[16,128,1024]{2,1,0:T(8,128)(2,1)} %all-to-all-done) | data formatting | bytes 8388608 | tf_op jit(solution)/shard_map/all_to_all | solution.py:75
  275.0 0.0 copy-start
  275.0 3.2 %convert_element_type.68 = f32[16,128,1024]{1,2,0:T(8,128)S(1)} convert(bf16[16,128,1024]{1,2,0:T(8,128)(2,1)} %copy.14) | non-fusion elementwise | flops 2097152 | bytes 12582912 | tf_op jit(solution)/shard_map/convert_element_type | solution.py:77
  278.2 0.3 copy-done
  278.5 2.5 fusion.2
  280.9 6.4 %copy.15 = bf16[1,128,16384]{2,1,0:T(8,128)(2,1)} copy(bf16[1,128,16384]{1,2,0:T(8,128)(2,1)} %fusion.2) | data formatting | bytes 8388608
Async XLA Ops:
  7.2 159.9 %reduce-scatter.2.cloned.1.call-start = ((), (), s32[]{:S(2)}) async-start(), calls=%async_computation.2 | async-start | bytes 4456448 | tf_op jit(solution)/shard_map/reduce_scatter | solution.py:65
  26.8 164.4 %copy-start.1 = (f32[128,1024]{1,0:T(8,128)S(1)}, f32[128,1024]{1,0:T(8,128)}, u32[]{:S(2)}) copy-start(f32[128,1024]{1,0:T(8,128)} %param.7) | copy-start | bytes 1572868
  209.8 58.8 %all-to-all-start = ((bf16[16,128,1024]{2,1,0:T(8,128)(2,1)}), bf16[16,128,1024]{2,1,0:T(8,128)(2,1)}, u32[]{:S(2)}, u32[]{:S(2)}) async-start(bf16[16,128,1024]{2,1,0:T(8,128)(2,1)} %stack.2), calls=%async_computation.1 | async-start | bytes 8388608 | tf_op jit(solution)/shard_map/all_to_all | solution.py:75
  275.0 3.4 %copy-start = (bf16[1,128,16384]{1,2,0:T(8,128)(2,1)S(1)}, bf16[1,128,16384]{1,2,0:T(8,128)(2,1)}, u32[]{:S(2)}) copy-start(bf16[1,128,16384]{1,2,0:T(8,128)(2,1)} %copy.10) | copy-start | bytes 12582916
Sparse Core Ops, SparseCore 0:
  84.6 82.4 reduce-scatter.1
